TPU v7x, 32 devices: a whole 2x2x4 slice. The times are simulated.
32 devices in a mesh: dp: 4 (over y, x), vocab: 8 (over z, core).
Axes of the slice: x: 2, y: 2, z: 4, core: 2. Of those that a mesh axis runs over, the one named last changes fastest.
Arguments:
- hidden: bfloat16 [256, 3072], P(('dp', 'vocab')), parts along dimension 0, may hold values from -60 to 60
- weight: bfloat16 [3072, 8192], P(None, 'vocab'), may hold values from -0.32421875 to 0.32421875
- targets: int32 [256], P('dp'), parts along dimension 0, may hold values from 0 to 8191
Outputs:
- loss: float32 [4], P('dp'), parts along dimension 0
- d_hidden: bfloat16 [256, 3072], P(('dp', 'vocab')), parts along dimension 0
- d_weight: bfloat16 [12288, 8192], P('dp', 'vocab'), parts along dimension 0
There are 4 independent parts, one for each index of `dp`. A program takes and returns all parts, laid end to end along the dimension named above; an argument that names none is the same for every part. Nothing has to cross between parts.
All inputs are finite; a program needn't handle non-finite values.
Results may differ from a plain program's by a relative error of at most 0.0035.
Values may be sent and summed in bfloat16 or wider, within the bound.
A program may use at most 64 MiB of HBM per device.

v0:
```python
import functools

import jax
import jax.numpy as jnp
from jax import lax
from jax.experimental import pallas as pl
from jax.experimental.pallas import tpu as pltpu
from jax.sharding import PartitionSpec as P

MESH = pl.DeviceIdType.MESH
F32 = jnp.float32
BF16 = jnp.bfloat16


def split(length, most, unit):
    for parts in range(most, 0, -1):
        if length % (parts * unit) == 0:
            return parts
    return 1


def remote(src, dst, send, recv, device):
    return pltpu.make_async_remote_copy(
        src_ref=src, dst_ref=dst, send_sem=send, recv_sem=recv, device_id={"vocab": device}, device_id_type=MESH
    )


def loss_kernel(
    n, h_hbm, w_hbm, t_hbm, dw_ref, dh_ref, loss_ref,
    h_ref, t_ref, aim_ref, hid_ref, turned_ref, g_ref, w_v, slots, e_v, stats, part, xbuf, outb, rbuf,
    in_sem, w_sem, ag_send, fw_send, ag_recv, st_send, st_recv, x_send, x_recv, rs_send, rs_recv,
):
    me = lax.axis_index("vocab")
    chips = n // 2
    chip, core = me // 2, me % 2
    partner = chip * 2 + (1 - core)
    rows, depth = h_ref.shape
    tokens, width = e_v.shape
    pieces, span = slots.shape[0], slots.shape[3]
    parts, wide = part.shape[0], part.shape[4]
    blocks = split(depth, 6, 256)
    tall = depth // blocks

    above = chips - 1 - chip

    def other(k):
        up = (above - k + chips) // chips
        return up * (chips - k) + (1 - up) * (k - 1 - above)

    takes = [pltpu.make_async_copy(h_hbm, h_ref, in_sem.at[0]), pltpu.make_async_copy(t_hbm, t_ref, in_sem.at[1])]
    for take in takes:
        take.start()
    loads = [
        pltpu.make_async_copy(w_hbm.at[pl.ds(a * span, span), :], w_v.at[pl.ds(a * span, span), :], w_sem.at[a])
        for a in range(pieces)
    ]
    for load in loads:
        load.start()

    barrier = pltpu.get_barrier_semaphore()
    for k in range(1, n):
        pl.semaphore_signal(barrier, inc=1, device_id={"vocab": lax.rem(me + k, n)}, device_id_type=MESH)
    for take in takes:
        take.wait()
    for a in range(pieces):
        slots[a, me] = h_ref[:, a * span:(a + 1) * span]
    aim_ref[...] = jnp.transpose(jnp.broadcast_to((t_ref[...] - me * width).astype(F32), (128, tokens)))
    pl.semaphore_wait(barrier, n - 1)

    sends = []
    for a in range(pieces):
        own = h_ref.at[:, pl.ds(a * span, span)]
        for k in range(chips):
            target = partner if k == 0 else other(k) * 2 + core
            copy = remote(own, slots.at[a, me], ag_send.at[a, k], ag_recv.at[a, me], target)
            copy.start()
            sends.append(copy)

    for a in range(pieces):
        for k in range(chips - 1, 0, -1):
            source = other(k) * 2 + core
            copy = remote(slots.at[a, source], slots.at[a, source], fw_send.at[a, k], ag_recv.at[a, source], partner)
            copy.wait_recv()
            copy.start()
            sends.append(copy)
        for k in range(chips):
            source = partner if k == 0 else other(k) * 2 + (1 - core)
            remote(slots.at[a, source], slots.at[a, source], fw_send.at[a, k], ag_recv.at[a, source], partner).wait_recv()
        for z in range(chips):
            both = jnp.concatenate([slots[a, 2 * z].astype(F32), slots[a, 2 * z + 1].astype(F32)], axis=0)
            hid_ref[2 * rows * z:2 * rows * (z + 1), a * span:(a + 1) * span] = both.astype(BF16)
        loads[a].wait()
        term = jnp.dot(
            hid_ref[:, a * span:(a + 1) * span], w_v[a * span:(a + 1) * span, :], preferred_element_type=F32
        )
        if a == 0:
            e_v[...] = term
        else:
            e_v[...] += term

    logits = e_v[...]
    hits = lax.broadcasted_iota(jnp.int32, (tokens, width), 1).astype(F32) == aim_ref[:, 0:1]
    local_top = jnp.max(logits, axis=1, keepdims=True)
    expo = jnp.exp(logits - local_top)
    local_total = jnp.sum(expo, axis=1, keepdims=True)
    local_picked = jnp.sum(jnp.where(hits, logits, 0.0), axis=1, keepdims=True)
    e_v[...] = expo
    lane = lax.broadcasted_iota(jnp.int32, (tokens, 128), 1)
    packed = jnp.where(lane == 0, local_top, jnp.where(lane == 1, local_total, local_picked))
    stats[me] = jnp.transpose(packed)[0:8, :]
    for k in range(1, n):
        copy = remote(stats.at[me], stats.at[me], st_send.at[k], st_recv.at[me], lax.rem(me + k, n))
        copy.start()
        sends.append(copy)
    for b in range(blocks):
        turned_ref[b * tall:(b + 1) * tall, :] = jnp.transpose(hid_ref[:, b * tall:(b + 1) * tall])
    for k in range(1, n):
        source = lax.rem(me + k, n)
        remote(stats.at[source], stats.at[source], st_send.at[k], st_recv.at[source], source).wait_recv()

    top = stats[0, 0:1, :]
    for k in range(1, n):
        top = jnp.maximum(top, stats[k, 0:1, :])
    total = jnp.zeros_like(top)
    picked = jnp.zeros_like(top)
    for k in range(n):
        total += stats[k, 1:2, :] * jnp.exp(stats[k, 0:1, :] - top)
        picked += stats[k, 2:3, :]
    loss_ref[...] = jnp.broadcast_to(jnp.sum(top + jnp.log(total) - picked, axis=1, keepdims=True) / tokens, loss_ref.shape)

    sub = lax.broadcasted_iota(jnp.int32, (128, tokens), 0)
    turned = jnp.transpose(jnp.where(sub == 0, top, total))
    factor = jnp.exp(local_top - turned[:, 0:1]) / turned[:, 1:2]
    grad = (e_v[...] * factor - hits.astype(F32)).astype(BF16)
    g_ref[...] = grad

    def pair_copy(j):
        return remote(part.at[j, 1 - core], xbuf.at[j], x_send.at[j], x_recv.at[j], partner)

    def group_copy(j, k):
        return remote(outb.at[j, other(k)], rbuf.at[j, chip], rs_send.at[j, k], rs_recv.at[j, chip], other(k) * 2 + core)

    def pass_on(j):
        pair_copy(j).wait_recv()
        for z in range(chips):
            outb[j, z] = (part[j, core, z] + xbuf[j, z]).astype(BF16)
        for k in range(1, chips):
            copy = group_copy(j, k)
            copy.start()
            sends.append(copy)

    for j in range(parts):
        term = lax.dot_general(
            g_ref[...], w_v[j * wide:(j + 1) * wide, :], (((1,), (1,)), ((), ())), preferred_element_type=F32
        )
        for z in range(chips):
            for half in range(2):
                at = (2 * z + half) * rows
                part[j, half, z] = term[at:at + rows, :]
        copy = pair_copy(j)
        copy.start()
        sends.append(copy)
        if j > 0:
            pass_on(j - 1)
    pass_on(parts - 1)
    for b in range(blocks):
        dw_ref[b * tall:(b + 1) * tall, :] = jnp.dot(
            turned_ref[b * tall:(b + 1) * tall, :], g_ref[...], preferred_element_type=F32
        ).astype(BF16)

    for j in range(parts):
        summed = part[j, core, chip] + xbuf[j, chip]
        for k in range(1, chips):
            source = other(k)
            remote(rbuf.at[j, source], rbuf.at[j, source], rs_send.at[j, k], rs_recv.at[j, source], source * 2 + core).wait_recv()
            summed += rbuf[j, source].astype(F32)
        dh_ref[:, j * wide:(j + 1) * wide] = summed.astype(BF16)

    for copy in sends:
        copy.wait_send()


def store_kernel(dw_v, dh_v, loss_v, dw_hbm, dh_hbm, loss_hbm, one_v, sem):
    one_v[...] = loss_v[0:1, 0:1]
    copies = []
    count = sem.shape[0] - 2
    tall = dw_v.shape[0] // count
    for b in range(count):
        at = pl.ds(b * tall, tall)
        copies.append(pltpu.make_async_copy(dw_v.at[at, :], dw_hbm.at[at, :], sem.at[2 + b]))
    copies.append(pltpu.make_async_copy(dh_v, dh_hbm, sem.at[0]))
    copies.append(pltpu.make_async_copy(one_v, loss_hbm, sem.at[1]))
    for copy in copies:
        copy.start()
    for copy in copies:
        copy.wait()


def body(n, hidden, weight, targets):
    rows, depth = hidden.shape
    width = weight.shape[1]
    tokens = rows * n
    chips = n // 2
    pieces = split(depth, 2, 256)
    parts = split(depth, 6, 256)
    span, wide = depth // pieces, depth // parts
    vmem = pl.BlockSpec(memory_space=pltpu.VMEM)
    dma = pltpu.SemaphoreType.DMA
    hbm = pl.BlockSpec(memory_space=pltpu.HBM)
    shared = (jax.ShapeDtypeStruct((depth, width), BF16), jax.ShapeDtypeStruct((rows, depth), BF16))
    tile = jax.ShapeDtypeStruct((8, 128), F32)
    held = pl.pallas_call(
        functools.partial(loss_kernel, n),
        out_shape=(*shared, tile),
        in_specs=[hbm, hbm, hbm],
        out_specs=(vmem, vmem, vmem),
        scratch_shapes=[
            pltpu.VMEM((rows, depth), BF16),
            pltpu.VMEM((1, tokens), jnp.int32),
            pltpu.VMEM((tokens, 128), F32),
            pltpu.VMEM((tokens, depth), BF16),
            pltpu.VMEM((depth, tokens), BF16),
            pltpu.VMEM((tokens, width), BF16),
            pltpu.VMEM((depth, width), BF16),
            pltpu.VMEM((pieces, n, rows, span), BF16),
            pltpu.VMEM((tokens, width), F32),
            pltpu.VMEM((n, 8, tokens), F32),
            pltpu.VMEM((parts, 2, chips, rows, wide), F32),
            pltpu.VMEM((parts, chips, rows, wide), F32),
            pltpu.VMEM((parts, chips, rows, wide), BF16),
            pltpu.VMEM((parts, chips, rows, wide), BF16),
            dma((2,)),
            dma((pieces,)),
            dma((pieces, chips)),
            dma((pieces, chips)),
            dma((pieces, n)),
            dma((n,)),
            dma((n,)),
            dma((parts,)),
            dma((parts,)),
            dma((parts, chips)),
            dma((parts, chips)),
        ],
        compiler_params=pltpu.CompilerParams(
            collective_id=0, has_side_effects=True, vmem_limit_bytes=45 * 1024 * 1024
        ),
    )(hidden, weight, targets.reshape(1, tokens))
    d_weight, d_hidden, loss = pl.pallas_call(
        store_kernel,
        out_shape=(*shared, jax.ShapeDtypeStruct((1, 1), F32)),
        in_specs=[vmem, vmem, vmem],
        out_specs=(hbm, hbm, hbm),
        scratch_shapes=[pltpu.VMEM((1, 1), F32), dma((2 + split(depth, 12, 16),))],
        compiler_params=pltpu.CompilerParams(vmem_limit_bytes=2 * 1024 * 1024),
    )(*held)
    return loss.reshape(1), d_hidden, d_weight


def solution(mesh):
    placed = (P(("dp", "vocab"), None), P(None, "vocab"), P("dp"))
    return jax.shard_map(
        functools.partial(body, mesh.shape["vocab"]),
        mesh=mesh,
        in_specs=placed,
        out_specs=(P("dp"), P(("dp", "vocab"), None), P("dp", "vocab")),
        check_vma=False,
    )
```

profile of v0, /device:TPU:0, one launch (start us, length us, event | category | flops | bytes accessed | tf_op | source)
XLA Modules:
  0.0 30.6 jit_solution(15074724574860486947)
XLA Ops:
  0.6 0.0 copy-start
  0.6 0.8 %copy-done = bf16[8,3072]{1,0:T(8,128)(2,1)S(1)} copy-done((bf16[8,3072]{1,0:T(8,128)(2,1)S(1)}, bf16[8,3072]{1,0:T(8,128)(2,1)}, u32[]{:S(2)}) %copy-start) | copy-done | bytes 49176
  1.4 0.0 copy-start.1
  1.4 0.7 %copy-done.1 = s32[64]{0:T(128)S(1)} copy-done((s32[64]{0:T(128)S(1)}, s32[64]{0:T(128)}, u32[]{:S(2)}) %copy-start.1) | copy-done | bytes 280
  2.1 25.7 %shard_map.58 = (bf16[3072,1024]{1,0:T(8,128)(2,1)S(1)}, bf16[8,3072]{1,0:T(8,128)(2,1)S(1)}, f32[8,128]{1,0:T(8,128)S(1)}) custom-call(bf16[8,3072]{1,0:T(8,128)(2,1)S(1)} %copy-done, bf16[3072,1024]{1,0:T(8,128)(2,1)} %w_hbm.1, s32[1,64]{1,0:T(1,128)S(1)} %bitcast.2), custom_call_target="tpu_custom_call" | custom-call | tf_op jit(solution)/shard_map/pallas_call | solution.py:212
  27.8 2.8 %shard_map.59 = (bf16[3072,1024]{1,0:T(8,128)(2,1)}, bf16[8,3072]{1,0:T(8,128)(2,1)}, f32[1,1]{1,0:T(1,128)}) custom-call(bf16[3072,1024]{1,0:T(8,128)(2,1)S(1)} %get-tuple-element.9.dw_v, bf16[8,3072]{1,0:T(8,128)(2,1)S(1)} %get-tuple-element.10.dh_v, f32[8,128]{1,0:T(8,128)S(1)} %get-tuple-element.11.loss_v), custom_call_target="tpu_custom_call" | custom-call | tf_op jit(solution)/shard_map/pallas_call | solution.py:248
Async XLA Ops:
  0.6 0.8 %copy-start = (bf16[8,3072]{1,0:T(8,128)(2,1)S(1)}, bf16[8,3072]{1,0:T(8,128)(2,1)}, u32[]{:S(2)}) copy-start(bf16[8,3072]{1,0:T(8,128)(2,1)} %h_hbm.1) | copy-start | bytes 147460
  1.4 0.7 %copy-start.1 = (s32[64]{0:T(128)S(1)}, s32[64]{0:T(128)}, u32[]{:S(2)}) copy-start(s32[64]{0:T(128)} %param.5) | copy-start | bytes 772
where the time goes:
time: 30.8 us; the launch traced here: 30.6 us
  Pallas kernels  28.5 us (93%)
  local copies, waits for them, and re-layouts  1.45 us (5%)
  between operations  0.65 us (2%)
    pallas_call x1, Pallas kernels, body(): pl.pallas_call(functools.partial(loss_kernel, n), out_shape=(*shared, til...  25.7 us
    pallas_call x1, Pallas kernels, body(): pl.pallas_call(store_kernel, out_shape=(*shared, jax.ShapeDtypeStruct((1,...  2.77 us
    unnamed x4, local copies, waits for them, and re-layouts  1.45 us

commit v1 on v0

v1 whole, which is shorter than its diff:
```python
import functools

import jax
import jax.numpy as jnp
from jax import lax
from jax.experimental import pallas as pl
from jax.experimental.pallas import tpu as pltpu
from jax.sharding import PartitionSpec as P

MESH = pl.DeviceIdType.MESH
F32 = jnp.float32
BF16 = jnp.bfloat16
ACROSS = (((1,), (1,)), ((), ()))
DOWN = (((0,), (0,)), ((), ()))


def split(length, most, unit):
    for parts in range(most, 0, -1):
        if length % (parts * unit) == 0:
            return parts
    return 1


def remote(src, dst, send, recv, device):
    return pltpu.make_async_remote_copy(
        src_ref=src, dst_ref=dst, send_sem=send, recv_sem=recv, device_id={"vocab": device}, device_id_type=MESH
    )


def loss_kernel(
    n, h_hbm, w_hbm, t_hbm, dw_ref, dh_ref, loss_ref,
    t_ref, aim_ref, hid_ref, g_ref, w_v, slots, e_v, stats, near, scale, mix, part, xbuf, outb, rbuf,
    goal, goal_in, goal_sum, goal_far,
    in_sem, w_sem, send_sem, ag_recv, fw_recv, recv_sem, x_recv,
):
    me = lax.axis_index("vocab")
    chips = n // 2
    chip, core = me // 2, me % 2
    partner = chip * 2 + (1 - core)
    pieces, rows, span = slots.shape[0], slots.shape[3], slots.shape[4]
    tokens, width = e_v.shape
    depth = w_v.shape[0]
    parts, wide = part.shape[0], part.shape[4]
    blocks = split(depth, 6, 256)
    tall = depth // blocks
    ag_send, fw_send, st_send, near_send, x_send, rs_send, goal_send, far_send = [send_sem.at[i] for i in range(8)]
    st_recv, near_recv, rs_recv, goal_recv, far_recv = [recv_sem.at[i] for i in range(5)]

    above = chips - 1 - chip

    def other(k):
        up = (above - k + chips) // chips
        return up * (chips - k) + (1 - up) * (k - 1 - above)

    takes = [
        pltpu.make_async_copy(h_hbm.at[:, pl.ds(a * span, span)], slots.at[a, core, chip], in_sem.at[a])
        for a in range(pieces)
    ]
    takes.append(pltpu.make_async_copy(t_hbm, t_ref, in_sem.at[pieces]))
    for take in takes:
        take.start()
    loads = [
        pltpu.make_async_copy(w_hbm.at[pl.ds(a * span, span), :], w_v.at[pl.ds(a * span, span), :], w_sem.at[a])
        for a in range(pieces)
    ]
    for load in loads:
        load.start()

    barrier = pltpu.get_barrier_semaphore()
    for k in range(1, n):
        pl.semaphore_signal(barrier, inc=1, device_id={"vocab": lax.rem(me + k, n)}, device_id_type=MESH)
    for take in takes:
        take.wait()
    aim_ref[...] = jnp.transpose(jnp.broadcast_to((t_ref[...] - me * width).astype(F32), (128, tokens)))
    pl.semaphore_wait(barrier, n - 1)

    for a in range(pieces):
        own = slots.at[a, core, chip]
        for k in range(1, chips):
            remote(own, own, ag_send, ag_recv.at[a], other(k) * 2 + core).start()

    hits = lax.broadcasted_iota(jnp.int32, (tokens, width), 1).astype(F32) == aim_ref[:, 0:1]
    g_ref[...] = hits.astype(F32).astype(BF16)
    for load in loads:
        load.wait()
    for j in range(parts):
        term = lax.dot_general(g_ref[...], w_v[j * wide:(j + 1) * wide, :], ACROSS, preferred_element_type=F32)
        for z in range(chips):
            for half in range(2):
                at = (2 * z + half) * rows
                goal[half, z, :, j * wide:(j + 1) * wide] = term[at:at + rows, :].astype(BF16)
    goal_copy = remote(goal.at[1 - core], goal_in, goal_send, goal_recv, partner)
    goal_copy.start()
    goal_copy.wait_recv()
    for z in range(chips):
        goal_sum[z] = (goal[core, z].astype(F32) + goal_in[z].astype(F32)).astype(BF16)
    for k in range(1, chips):
        remote(goal_sum.at[other(k)], goal_far.at[chip], far_send, far_recv, other(k) * 2 + core).start()

    def finish(a):
        remote(slots.at[a, 1 - core], slots.at[a, 1 - core], fw_send, fw_recv.at[a], partner).wait_recv()
        for z in range(chips):
            both = jnp.concatenate([slots[a, 0, z].astype(F32), slots[a, 1, z].astype(F32)], axis=0)
            hid_ref[2 * rows * z:2 * rows * (z + 1), a * span:(a + 1) * span] = both.astype(BF16)
        term = jnp.dot(
            hid_ref[:, a * span:(a + 1) * span], w_v[a * span:(a + 1) * span, :], preferred_element_type=F32
        )
        if a == 0:
            e_v[...] = term
        else:
            e_v[...] += term

    for a in range(pieces):
        there = slots.at[a, core, pl.ds(0, chips - 1)]
        remote(there, there, ag_send, ag_recv.at[a], partner).wait_recv()
        remote(slots.at[a, core], slots.at[a, core], fw_send, fw_recv.at[a], partner).start()
        if a > 0:
            finish(a - 1)
    finish(pieces - 1)

    logits = e_v[...]
    hits = lax.broadcasted_iota(jnp.int32, (tokens, width), 1).astype(F32) == aim_ref[:, 0:1]
    local_top = jnp.max(logits, axis=1, keepdims=True)
    expo = jnp.exp(logits - local_top)
    e_v[...] = expo
    g_ref[...] = jnp.where(hits, 0.0, expo).astype(BF16)
    local_total = jnp.sum(expo, axis=1, keepdims=True)
    local_picked = jnp.sum(jnp.where(hits, logits, 0.0), axis=1, keepdims=True)
    lane = lax.broadcasted_iota(jnp.int32, (tokens, 128), 1)
    packed = jnp.where(lane == 0, local_top, jnp.where(lane == 1, local_total, local_picked))
    near[0] = packed
    near_copy = remote(near.at[0], near.at[1], near_send, near_recv, partner)
    near_copy.start()
    stats[me] = jnp.transpose(packed)[0:8, :]
    for k in range(1, n):
        remote(stats.at[me], stats.at[me], st_send, st_recv, lax.rem(me + k, n)).start()

    def pair_copy(j):
        return remote(part.at[j, 1 - core], xbuf.at[j], x_send, x_recv.at[j], partner)

    def chip_sum(j, z):
        return (
            part[j, core, z] * scale[0, core, z][:, 0:1] + xbuf[j, z] * scale[1, core, z][:, 0:1]
        )

    def pass_on(j):
        pair_copy(j).wait_recv()
        for z in range(chips):
            outb[j, z] = chip_sum(j, z).astype(BF16)
        for k in range(1, chips):
            remote(outb.at[j, other(k)], rbuf.at[j, chip], rs_send, rs_recv, other(k) * 2 + core).start()

    for j in range(parts):
        term = lax.dot_general(g_ref[...], w_v[j * wide:(j + 1) * wide, :], ACROSS, preferred_element_type=F32)
        for z in range(chips):
            for half in range(2):
                at = (2 * z + half) * rows
                part[j, half, z] = term[at:at + rows, :]
        pair_copy(j).start()
        if j == 0:
            near_copy.wait_recv()
            near_top = near[1][:, 0:1]
            chip_top = jnp.maximum(local_top, near_top)
            for i, own in enumerate((local_top, near_top)):
                spread = jnp.broadcast_to(jnp.exp(own - chip_top), (tokens, 128))
                for z in range(chips):
                    for half in range(2):
                        at = (2 * z + half) * rows
                        scale[i, half, z] = spread[at:at + rows, :]
        else:
            pass_on(j - 1)
    pass_on(parts - 1)

    remote(stats.at[pl.ds(0, n - 1)], stats.at[pl.ds(0, n - 1)], st_send, st_recv, partner).wait_recv()

    top = stats[0, 0:1, :]
    for k in range(1, n):
        top = jnp.maximum(top, stats[k, 0:1, :])
    total = jnp.zeros_like(top)
    picked = jnp.zeros_like(top)
    for k in range(n):
        total += stats[k, 1:2, :] * jnp.exp(stats[k, 0:1, :] - top)
        picked += stats[k, 2:3, :]
    loss_ref[...] = jnp.broadcast_to(jnp.sum(top + jnp.log(total) - picked, axis=1, keepdims=True) / tokens, loss_ref.shape)

    sub = lax.broadcasted_iota(jnp.int32, (128, tokens), 0)
    turned = jnp.where(sub == chips, jnp.exp(picked - top) / total - 1.0, jnp.where(sub == chips + 1, top, total))
    for z in range(chips):
        chip_top = jnp.maximum(stats[2 * z, 0:1, :], stats[2 * z + 1, 0:1, :])
        turned = jnp.where(sub == z, jnp.exp(chip_top - top) / total, turned)
    turned = jnp.transpose(turned)
    for k in range(n):
        mix[k] = turned[k * rows:(k + 1) * rows, :]
    factor = jnp.exp(local_top - turned[:, chips + 1:chips + 2]) / turned[:, chips + 2:chips + 3]
    hits = lax.broadcasted_iota(jnp.int32, (tokens, width), 1).astype(F32) == aim_ref[:, 0:1]
    g_ref[...] = (e_v[...] * factor - hits.astype(F32)).astype(BF16)

    for b in range(blocks):
        dw_ref[b * tall:(b + 1) * tall, :] = lax.dot_general(
            hid_ref[:, b * tall:(b + 1) * tall], g_ref[...], DOWN, preferred_element_type=F32
        ).astype(BF16)

    mine = mix[me]
    far = goal_far.at[pl.ds(0, chips - 1)]
    remote(far, far, far_send, far_recv, partner).wait_recv()
    there = rbuf.at[:, pl.ds(0, chips - 1)]
    remote(there, there, rs_send, rs_recv, partner).wait_recv()
    own_scale = mix[me]
    lanes = lax.broadcasted_iota(jnp.int32, (rows, 128), 1)
    own_scale = jnp.sum(jnp.where(lanes == chip, own_scale, 0.0), axis=1, keepdims=True)
    for j in range(parts):
        goals = goal_sum[chip, :, j * wide:(j + 1) * wide].astype(F32)
        summed = chip_sum(j, chip) * own_scale
        for k in range(1, chips):
            source = other(k)
            weight = jnp.sum(jnp.where(lanes == source, mine, 0.0), axis=1, keepdims=True)
            summed += rbuf[j, source].astype(F32) * weight
            goals += goal_far[source, :, j * wide:(j + 1) * wide].astype(F32)
        dh_ref[:, j * wide:(j + 1) * wide] = (summed + goals * mine[:, chips:chips + 1]).astype(BF16)

    for ref, sem in (
        (slots.at[:, 0, pl.ds(0, chips - 1)], ag_send), (slots.at[:, 0], fw_send), (stats.at[pl.ds(0, n - 1)], st_send),
        (near.at[0], near_send), (xbuf, x_send), (there, rs_send), (goal_in, goal_send), (far, far_send),
    ):
        remote(ref, ref, sem, st_recv, partner).wait_send()


def store_kernel(dw_v, dh_v, loss_v, dw_hbm, dh_hbm, loss_hbm, one_v, sem):
    one_v[...] = loss_v[0:1, 0:1]
    copies = []
    count = sem.shape[0] - 2
    tall = dw_v.shape[0] // count
    for b in range(count):
        at = pl.ds(b * tall, tall)
        copies.append(pltpu.make_async_copy(dw_v.at[at, :], dw_hbm.at[at, :], sem.at[2 + b]))
    copies.append(pltpu.make_async_copy(dh_v, dh_hbm, sem.at[0]))
    copies.append(pltpu.make_async_copy(one_v, loss_hbm, sem.at[1]))
    for copy in copies:
        copy.start()
    for copy in copies:
        copy.wait()


def body(n, hidden, weight, targets):
    rows, depth = hidden.shape
    width = weight.shape[1]
    tokens = rows * n
    chips = n // 2
    pieces = split(depth, 4, 256)
    parts = split(depth, 6, 256)
    span, wide = depth // pieces, depth // parts
    vmem = pl.BlockSpec(memory_space=pltpu.VMEM)
    dma = pltpu.SemaphoreType.DMA
    hbm = pl.BlockSpec(memory_space=pltpu.HBM)
    shared = (jax.ShapeDtypeStruct((depth, width), BF16), jax.ShapeDtypeStruct((rows, depth), BF16))
    tile = jax.ShapeDtypeStruct((8, 128), F32)
    held = pl.pallas_call(
        functools.partial(loss_kernel, n),
        out_shape=(*shared, tile),
        in_specs=[hbm, hbm, hbm],
        out_specs=(vmem, vmem, vmem),
        scratch_shapes=[
            pltpu.VMEM((1, tokens), jnp.int32),
            pltpu.VMEM((tokens, 128), F32),
            pltpu.VMEM((tokens, depth), BF16),
            pltpu.VMEM((tokens, width), BF16),
            pltpu.VMEM((depth, width), BF16),
            pltpu.VMEM((pieces, 2, chips, rows, span), BF16),
            pltpu.VMEM((tokens, width), F32),
            pltpu.VMEM((n, 8, tokens), F32),
            pltpu.VMEM((2, tokens, 128), F32),
            pltpu.VMEM((2, 2, chips, rows, 128), F32),
            pltpu.VMEM((n, rows, 128), F32),
            pltpu.VMEM((parts, 2, chips, rows, wide), F32),
            pltpu.VMEM((parts, chips, rows, wide), F32),
            pltpu.VMEM((parts, chips, rows, wide), BF16),
            pltpu.VMEM((parts, chips, rows, wide), BF16),
            pltpu.VMEM((2, chips, rows, depth), BF16),
            pltpu.VMEM((chips, rows, depth), BF16),
            pltpu.VMEM((chips, rows, depth), BF16),
            pltpu.VMEM((chips, rows, depth), BF16),
            dma((pieces + 1,)),
            dma((pieces,)),
            dma((8,)),
            dma((pieces,)),
            dma((pieces,)),
            dma((5,)),
            dma((parts,)),
        ],
        compiler_params=pltpu.CompilerParams(
            collective_id=0, has_side_effects=True, vmem_limit_bytes=45 * 1024 * 1024
        ),
    )(*[pltpu.with_memory_space_constraint(x, pltpu.HBM) for x in (hidden, weight, targets.reshape(1, tokens))])
    d_weight, d_hidden, loss = pl.pallas_call(
        store_kernel,
        out_shape=(*shared, jax.ShapeDtypeStruct((1, 1), F32)),
        in_specs=[vmem, vmem, vmem],
        out_specs=(hbm, hbm, hbm),
        scratch_shapes=[pltpu.VMEM((1, 1), F32), dma((2 + split(depth, 12, 16),))],
        compiler_params=pltpu.CompilerParams(vmem_limit_bytes=2 * 1024 * 1024),
    )(*held)
    return loss.reshape(1), d_hidden, d_weight


def solution(mesh):
    placed = (P(("dp", "vocab"), None), P(None, "vocab"), P("dp"))
    return jax.shard_map(
        functools.partial(body, mesh.shape["vocab"]),
        mesh=mesh,
        in_specs=placed,
        out_specs=(P("dp"), P(("dp", "vocab"), None), P("dp", "vocab")),
        check_vma=False,
    )
```

time: 30.8 us -> 27.2 us (0.88)
  Pallas kernels: 28.5 us -> 26.4 us
  local copies, waits for them, and re-layouts: 1.45 us -> 0 us
    pallas_call x1, Pallas kernels: 25.7 us -> 23.6 us  [body(): pl.pallas_call(functools.partial(loss_kernel, n), out_shape=(*shared, til...]
    unnamed x4 -> x0, local copies, waits for them, and re-layouts: 1.45 us -> none
where the time goes in v1:
time: 27.2 us; the launch traced here: 27.1 us
  Pallas kernels  26.4 us (97%)
  between operations  0.64 us (2%)
    pallas_call x1, Pallas kernels, body(): pl.pallas_call(functools.partial(loss_kernel, n), out_shape=(*shared, til...  23.6 us
    pallas_call x1, Pallas kernels, body(): pl.pallas_call(store_kernel, out_shape=(*shared, jax.ShapeDtypeStruct((1,...  2.77 us

profile of v1, /device:TPU:0, one launch (start us, length us, event | category | flops | bytes accessed | tf_op | source)
XLA Modules:
  0.0 27.1 jit_solution(14328593702019323590)
XLA Ops:
  0.6 23.6 %shard_map.58 = (bf16[3072,1024]{1,0:T(8,128)(2,1)S(1)}, bf16[8,3072]{1,0:T(8,128)(2,1)S(1)}, f32[8,128]{1,0:T(8,128)S(1)}) custom-call(bf16[8,3072]{1,0:T(8,128)(2,1)} %h_hbm.1, bf16[3072,1024]{1,0:T(8,128)(2,1)} %w_hbm.1, s32[1,64]{1,0:T(1,128)} %bitcast.2), custom_call_target="tpu_custom_call" | custom-call | tf_op jit(solution)/shard_map/pallas_call | solution.py:257
  24.3 2.8 %shard_map.59 = (bf16[3072,1024]{1,0:T(8,128)(2,1)}, bf16[8,3072]{1,0:T(8,128)(2,1)}, f32[1,1]{1,0:T(1,128)}) custom-call(bf16[3072,1024]{1,0:T(8,128)(2,1)S(1)} %get-tuple-element.9.dw_v, bf16[8,3072]{1,0:T(8,128)(2,1)S(1)} %get-tuple-element.10.dh_v, f32[8,128]{1,0:T(8,128)S(1)} %get-tuple-element.11.loss_v), custom_call_target="tpu_custom_call" | custom-call | tf_op jit(solution)/shard_map/pallas_call | solution.py:294

commit v2 on v1

--- a/solution.py
+++ b/solution.py
@@ -21,6 +21,12 @@
     return 1
 
 
+def plan(units):
+    if units == 12:
+        return [6, 6], 1, [[], [0, 1]]
+    return [1] * units, 1, [[] if j == 0 else [j - 1] for j in range(units - 1)] + [[units - 2, units - 1] if units > 1 else [0]]
+
+
 def remote(src, dst, send, recv, device):
     return pltpu.make_async_remote_copy(
         src_ref=src, dst_ref=dst, send_sem=send, recv_sem=recv, device_id={"vocab": device}, device_id_type=MESH
@@ -28,7 +34,7 @@
 
 
 def loss_kernel(
-    n, h_hbm, w_hbm, t_hbm, dw_ref, dh_ref, loss_ref,
+    n, widths, turn, after, h_hbm, w_hbm, t_hbm, dw_ref, dh_ref, loss_ref,
     t_ref, aim_ref, hid_ref, g_ref, w_v, slots, e_v, stats, near, scale, mix, part, xbuf, outb, rbuf,
     goal, goal_in, goal_sum, goal_far,
     in_sem, w_sem, send_sem, ag_recv, fw_recv, recv_sem, x_recv,
@@ -40,9 +46,9 @@
     pieces, rows, span = slots.shape[0], slots.shape[3], slots.shape[4]
     tokens, width = e_v.shape
     depth = w_v.shape[0]
-    parts, wide = part.shape[0], part.shape[4]
     blocks = split(depth, 6, 256)
     tall = depth // blocks
+    starts = [sum(widths[:j]) for j in range(len(widths))]
     ag_send, fw_send, st_send, near_send, x_send, rs_send, goal_send, far_send = [send_sem.at[i] for i in range(8)]
     st_recv, near_recv, rs_recv, goal_recv, far_recv = [recv_sem.at[i] for i in range(5)]
 
@@ -63,14 +69,14 @@
         pltpu.make_async_copy(w_hbm.at[pl.ds(a * span, span), :], w_v.at[pl.ds(a * span, span), :], w_sem.at[a])
         for a in range(pieces)
     ]
-    for load in loads:
-        load.start()
 
     barrier = pltpu.get_barrier_semaphore()
     for k in range(1, n):
         pl.semaphore_signal(barrier, inc=1, device_id={"vocab": lax.rem(me + k, n)}, device_id_type=MESH)
     for take in takes:
         take.wait()
+    for load in loads:
+        load.start()
     aim_ref[...] = jnp.transpose(jnp.broadcast_to((t_ref[...] - me * width).astype(F32), (128, tokens)))
     pl.semaphore_wait(barrier, n - 1)
 
@@ -83,12 +89,12 @@
     g_ref[...] = hits.astype(F32).astype(BF16)
     for load in loads:
         load.wait()
-    for j in range(parts):
-        term = lax.dot_general(g_ref[...], w_v[j * wide:(j + 1) * wide, :], ACROSS, preferred_element_type=F32)
+    for b in range(blocks):
+        term = lax.dot_general(g_ref[...], w_v[b * tall:(b + 1) * tall, :], ACROSS, preferred_element_type=F32)
         for z in range(chips):
             for half in range(2):
                 at = (2 * z + half) * rows
-                goal[half, z, :, j * wide:(j + 1) * wide] = term[at:at + rows, :].astype(BF16)
+                goal[half, z, :, b * tall:(b + 1) * tall] = term[at:at + rows, :].astype(BF16)
     goal_copy = remote(goal.at[1 - core], goal_in, goal_send, goal_recv, partner)
     goal_copy.start()
     goal_copy.wait_recv()
@@ -136,28 +142,23 @@
         remote(stats.at[me], stats.at[me], st_send, st_recv, lax.rem(me + k, n)).start()
 
     def pair_copy(j):
-        return remote(part.at[j, 1 - core], xbuf.at[j], x_send, x_recv.at[j], partner)
-
-    def chip_sum(j, z):
-        return (
-            part[j, core, z] * scale[0, core, z][:, 0:1] + xbuf[j, z] * scale[1, core, z][:, 0:1]
-        )
+        at = pl.ds(starts[j], widths[j])
+        return remote(part.at[1 - core, :, :, at], xbuf.at[:, :, at], x_send, x_recv.at[j], partner)
+
+    def chip_sum(z, at):
+        return part[core, z, :, at] * scale[0, core, z][:, 0:1] + xbuf[z, :, at] * scale[1, core, z][:, 0:1]
 
     def pass_on(j):
+        at = slice(starts[j], starts[j] + widths[j])
         pair_copy(j).wait_recv()
         for z in range(chips):
-            outb[j, z] = chip_sum(j, z).astype(BF16)
+            outb[z, :, at] = chip_sum(z, at).astype(BF16)
+        at = pl.ds(starts[j], widths[j])
         for k in range(1, chips):
-            remote(outb.at[j, other(k)], rbuf.at[j, chip], rs_send, rs_recv, other(k) * 2 + core).start()
-
-    for j in range(parts):
-        term = lax.dot_general(g_ref[...], w_v[j * wide:(j + 1) * wide, :], ACROSS, preferred_element_type=F32)
-        for z in range(chips):
-            for half in range(2):
-                at = (2 * z + half) * rows
-                part[j, half, z] = term[at:at + rows, :]
-        pair_copy(j).start()
-        if j == 0:
+            remote(outb.at[other(k), :, at], rbuf.at[chip, :, at], rs_send, rs_recv, other(k) * 2 + core).start()
+
+    for j in range(len(widths)):
+        if j == turn:
             near_copy.wait_recv()
             near_top = near[1][:, 0:1]
             chip_top = jnp.maximum(local_top, near_top)
@@ -167,9 +168,16 @@
                     for half in range(2):
                         at = (2 * z + half) * rows
                         scale[i, half, z] = spread[at:at + rows, :]
-        else:
-            pass_on(j - 1)
-    pass_on(parts - 1)
+        term = lax.dot_general(
+            g_ref[...], w_v[starts[j]:starts[j] + widths[j], :], ACROSS, preferred_element_type=F32
+        )
+        for z in range(chips):
+            for half in range(2):
+                at = (2 * z + half) * rows
+                part[half, z, :, starts[j]:starts[j] + widths[j]] = term[at:at + rows, :]
+        pair_copy(j).start()
+        for i in after[j]:
+            pass_on(i)
 
     remote(stats.at[pl.ds(0, n - 1)], stats.at[pl.ds(0, n - 1)], st_send, st_recv, partner).wait_recv()
 
@@ -203,20 +211,21 @@
     mine = mix[me]
     far = goal_far.at[pl.ds(0, chips - 1)]
     remote(far, far, far_send, far_recv, partner).wait_recv()
-    there = rbuf.at[:, pl.ds(0, chips - 1)]
+    there = rbuf.at[pl.ds(0, chips - 1)]
     remote(there, there, rs_send, rs_recv, partner).wait_recv()
-    own_scale = mix[me]
     lanes = lax.broadcasted_iota(jnp.int32, (rows, 128), 1)
-    own_scale = jnp.sum(jnp.where(lanes == chip, own_scale, 0.0), axis=1, keepdims=True)
-    for j in range(parts):
-        goals = goal_sum[chip, :, j * wide:(j + 1) * wide].astype(F32)
-        summed = chip_sum(j, chip) * own_scale
+    share = [
+        jnp.sum(jnp.where(lanes == z, mine, 0.0), axis=1, keepdims=True)
+        for z in [chip] + [other(k) for k in range(1, chips)]
+    ]
+    for b in range(blocks):
+        at = slice(b * tall, (b + 1) * tall)
+        goals = goal_sum[chip, :, at].astype(F32)
+        summed = chip_sum(chip, at) * share[0]
         for k in range(1, chips):
-            source = other(k)
-            weight = jnp.sum(jnp.where(lanes == source, mine, 0.0), axis=1, keepdims=True)
-            summed += rbuf[j, source].astype(F32) * weight
-            goals += goal_far[source, :, j * wide:(j + 1) * wide].astype(F32)
-        dh_ref[:, j * wide:(j + 1) * wide] = (summed + goals * mine[:, chips:chips + 1]).astype(BF16)
+            summed += rbuf[other(k), :, at].astype(F32) * share[k]
+            goals += goal_far[other(k), :, at].astype(F32)
+        dh_ref[:, at] = (summed + goals * mine[:, chips:chips + 1]).astype(BF16)
 
     for ref, sem in (
         (slots.at[:, 0, pl.ds(0, chips - 1)], ag_send), (slots.at[:, 0], fw_send), (stats.at[pl.ds(0, n - 1)], st_send),
@@ -246,16 +255,18 @@
     width = weight.shape[1]
     tokens = rows * n
     chips = n // 2
-    pieces = split(depth, 4, 256)
-    parts = split(depth, 6, 256)
-    span, wide = depth // pieces, depth // parts
+    pieces = split(depth, 3, 256)
+    unit = depth // split(depth, 12, 128)
+    widths, turn, after = plan(depth // unit)
+    widths = [w * unit for w in widths]
+    span = depth // pieces
     vmem = pl.BlockSpec(memory_space=pltpu.VMEM)
     dma = pltpu.SemaphoreType.DMA
     hbm = pl.BlockSpec(memory_space=pltpu.HBM)
     shared = (jax.ShapeDtypeStruct((depth, width), BF16), jax.ShapeDtypeStruct((rows, depth), BF16))
     tile = jax.ShapeDtypeStruct((8, 128), F32)
     held = pl.pallas_call(
-        functools.partial(loss_kernel, n),
+        functools.partial(loss_kernel, n, widths, turn, after),
         out_shape=(*shared, tile),
         in_specs=[hbm, hbm, hbm],
         out_specs=(vmem, vmem, vmem),
@@ -271,10 +282,10 @@
             pltpu.VMEM((2, tokens, 128), F32),
             pltpu.VMEM((2, 2, chips, rows, 128), F32),
             pltpu.VMEM((n, rows, 128), F32),
-            pltpu.VMEM((parts, 2, chips, rows, wide), F32),
-            pltpu.VMEM((parts, chips, rows, wide), F32),
-            pltpu.VMEM((parts, chips, rows, wide), BF16),
-            pltpu.VMEM((parts, chips, rows, wide), BF16),
+            pltpu.VMEM((2, chips, rows, depth), F32),
+            pltpu.VMEM((chips, rows, depth), F32),
+            pltpu.VMEM((chips, rows, depth), BF16),
+            pltpu.VMEM((chips, rows, depth), BF16),
             pltpu.VMEM((2, chips, rows, depth), BF16),
             pltpu.VMEM((chips, rows, depth), BF16),
             pltpu.VMEM((chips, rows, depth), BF16),
@@ -285,7 +296,7 @@
             dma((pieces,)),
             dma((pieces,)),
             dma((5,)),
-            dma((parts,)),
+            dma((len(widths),)),
         ],
         compiler_params=pltpu.CompilerParams(
             collective_id=0, has_side_effects=True, vmem_limit_bytes=45 * 1024 * 1024

time: 27.2 us -> 25.2 us (0.926)
  Pallas kernels: 26.4 us -> 24.3 us
    pallas_call x1, Pallas kernels: 23.6 us -> 21.5 us  [body(): pl.pallas_call(functools.partial(loss_kernel, n, widths, turn, after), ou...]
where the time goes in v2:
time: 25.2 us; the launch traced here: 24.9 us
  Pallas kernels  24.3 us (96%)
  between operations  0.64 us (3%)
    pallas_call x1, Pallas kernels, body(): pl.pallas_call(functools.partial(loss_kernel, n, widths, turn, after), ou...  21.5 us
    pallas_call x1, Pallas kernels, body(): pl.pallas_call(store_kernel, out_shape=(*shared, jax.ShapeDtypeStruct((1,...  2.77 us

profile of v2, /device:TPU:0, one launch (start us, length us, event | category | flops | bytes accessed | tf_op | source)
XLA Modules:
  0.0 24.9 jit_solution(1539778898567568259)
XLA Ops:
  0.6 21.5 %shard_map.58 = (bf16[3072,1024]{1,0:T(8,128)(2,1)S(1)}, bf16[8,3072]{1,0:T(8,128)(2,1)S(1)}, f32[8,128]{1,0:T(8,128)S(1)}) custom-call(bf16[8,3072]{1,0:T(8,128)(2,1)} %h_hbm.1, bf16[3072,1024]{1,0:T(8,128)(2,1)} %w_hbm.1, s32[1,64]{1,0:T(1,128)} %bitcast.2), custom_call_target="tpu_custom_call" | custom-call | tf_op jit(solution)/shard_map/pallas_call | solution.py:268
  22.1 2.8 %shard_map.59 = (bf16[3072,1024]{1,0:T(8,128)(2,1)}, bf16[8,3072]{1,0:T(8,128)(2,1)}, f32[1,1]{1,0:T(1,128)}) custom-call(bf16[3072,1024]{1,0:T(8,128)(2,1)S(1)} %get-tuple-element.9.dw_v, bf16[8,3072]{1,0:T(8,128)(2,1)S(1)} %get-tuple-element.10.dh_v, f32[8,128]{1,0:T(8,128)S(1)} %get-tuple-element.11.loss_v), custom_call_target="tpu_custom_call" | custom-call | tf_op jit(solution)/shard_map/pallas_call | solution.py:305

commit v3 on v2

--- a/solution.py
+++ b/solution.py
@@ -42,7 +42,8 @@
     me = lax.axis_index("vocab")
     chips = n // 2
     chip, core = me // 2, me % 2
-    partner = chip * 2 + (1 - core)
+    away = 1 - core
+    partner = chip * 2 + away
     pieces, rows, span = slots.shape[0], slots.shape[3], slots.shape[4]
     tokens, width = e_v.shape
     depth = w_v.shape[0]
@@ -83,7 +84,8 @@
     for a in range(pieces):
         own = slots.at[a, core, chip]
         for k in range(1, chips):
-            remote(own, own, ag_send, ag_recv.at[a], other(k) * 2 + core).start()
+            remote(own, own, ag_send, ag_recv.at[a], other(k) * 2 + away).start()
+        remote(own, own, ag_send, fw_recv.at[a], partner).start()
 
     hits = lax.broadcasted_iota(jnp.int32, (tokens, width), 1).astype(F32) == aim_ref[:, 0:1]
     g_ref[...] = hits.astype(F32).astype(BF16)
@@ -95,16 +97,17 @@
             for half in range(2):
                 at = (2 * z + half) * rows
                 goal[half, z, :, b * tall:(b + 1) * tall] = term[at:at + rows, :].astype(BF16)
-    goal_copy = remote(goal.at[1 - core], goal_in, goal_send, goal_recv, partner)
+    goal_copy = remote(goal.at[core], goal_in, goal_send, goal_recv, partner)
     goal_copy.start()
     goal_copy.wait_recv()
     for z in range(chips):
-        goal_sum[z] = (goal[core, z].astype(F32) + goal_in[z].astype(F32)).astype(BF16)
+        goal_sum[z] = (goal[away, z].astype(F32) + goal_in[z].astype(F32)).astype(BF16)
     for k in range(1, chips):
-        remote(goal_sum.at[other(k)], goal_far.at[chip], far_send, far_recv, other(k) * 2 + core).start()
+        remote(goal_sum.at[other(k)], goal_far.at[chip], far_send, far_recv, other(k) * 2 + away).start()
+    remote(goal_sum.at[chip], goal_far.at[chip], far_send, far_recv, partner).start()
 
     def finish(a):
-        remote(slots.at[a, 1 - core], slots.at[a, 1 - core], fw_send, fw_recv.at[a], partner).wait_recv()
+        remote(slots.at[a, core], slots.at[a, core], fw_send, fw_recv.at[a], partner).wait_recv()
         for z in range(chips):
             both = jnp.concatenate([slots[a, 0, z].astype(F32), slots[a, 1, z].astype(F32)], axis=0)
             hid_ref[2 * rows * z:2 * rows * (z + 1), a * span:(a + 1) * span] = both.astype(BF16)
@@ -117,9 +120,11 @@
             e_v[...] += term
 
     for a in range(pieces):
-        there = slots.at[a, core, pl.ds(0, chips - 1)]
+        there = slots.at[a, away, pl.ds(0, chips - 1)]
         remote(there, there, ag_send, ag_recv.at[a], partner).wait_recv()
-        remote(slots.at[a, core], slots.at[a, core], fw_send, fw_recv.at[a], partner).start()
+        for k in range(1, chips):
+            there = slots.at[a, away, other(k)]
+            remote(there, there, fw_send, fw_recv.at[a], partner).start()
         if a > 0:
             finish(a - 1)
     finish(pieces - 1)
@@ -143,10 +148,10 @@
 
     def pair_copy(j):
         at = pl.ds(starts[j], widths[j])
-        return remote(part.at[1 - core, :, :, at], xbuf.at[:, :, at], x_send, x_recv.at[j], partner)
+        return remote(part.at[core, :, :, at], xbuf.at[:, :, at], x_send, x_recv.at[j], partner)
 
     def chip_sum(z, at):
-        return part[core, z, :, at] * scale[0, core, z][:, 0:1] + xbuf[z, :, at] * scale[1, core, z][:, 0:1]
+        return part[away, z, :, at] * scale[0, away, z][:, 0:1] + xbuf[z, :, at] * scale[1, away, z][:, 0:1]
 
     def pass_on(j):
         at = slice(starts[j], starts[j] + widths[j])
@@ -155,7 +160,8 @@
             outb[z, :, at] = chip_sum(z, at).astype(BF16)
         at = pl.ds(starts[j], widths[j])
         for k in range(1, chips):
-            remote(outb.at[other(k), :, at], rbuf.at[chip, :, at], rs_send, rs_recv, other(k) * 2 + core).start()
+            remote(outb.at[other(k), :, at], rbuf.at[chip, :, at], rs_send, rs_recv, other(k) * 2 + away).start()
+        remote(outb.at[chip, :, at], rbuf.at[chip, :, at], rs_send, rs_recv, partner).start()
 
     for j in range(len(widths)):
         if j == turn:
@@ -209,27 +215,20 @@
         ).astype(BF16)
 
     mine = mix[me]
-    far = goal_far.at[pl.ds(0, chips - 1)]
-    remote(far, far, far_send, far_recv, partner).wait_recv()
-    there = rbuf.at[pl.ds(0, chips - 1)]
-    remote(there, there, rs_send, rs_recv, partner).wait_recv()
-    lanes = lax.broadcasted_iota(jnp.int32, (rows, 128), 1)
-    share = [
-        jnp.sum(jnp.where(lanes == z, mine, 0.0), axis=1, keepdims=True)
-        for z in [chip] + [other(k) for k in range(1, chips)]
-    ]
+    remote(goal_far, goal_far, far_send, far_recv, partner).wait_recv()
+    remote(rbuf, rbuf, rs_send, rs_recv, partner).wait_recv()
     for b in range(blocks):
         at = slice(b * tall, (b + 1) * tall)
-        goals = goal_sum[chip, :, at].astype(F32)
-        summed = chip_sum(chip, at) * share[0]
-        for k in range(1, chips):
-            summed += rbuf[other(k), :, at].astype(F32) * share[k]
-            goals += goal_far[other(k), :, at].astype(F32)
+        goals = jnp.zeros((rows, tall), F32)
+        summed = jnp.zeros((rows, tall), F32)
+        for z in range(chips):
+            summed += rbuf[z, :, at].astype(F32) * mine[:, z:z + 1]
+            goals += goal_far[z, :, at].astype(F32)
         dh_ref[:, at] = (summed + goals * mine[:, chips:chips + 1]).astype(BF16)
 
     for ref, sem in (
-        (slots.at[:, 0, pl.ds(0, chips - 1)], ag_send), (slots.at[:, 0], fw_send), (stats.at[pl.ds(0, n - 1)], st_send),
-        (near.at[0], near_send), (xbuf, x_send), (there, rs_send), (goal_in, goal_send), (far, far_send),
+        (slots.at[:, 0], ag_send), (slots.at[:, 0, pl.ds(0, chips - 1)], fw_send), (stats.at[pl.ds(0, n - 1)], st_send),
+        (near.at[0], near_send), (xbuf, x_send), (rbuf, rs_send), (goal_in, goal_send), (goal_far, far_send),
     ):
         remote(ref, ref, sem, st_recv, partner).wait_send()
 

time: 25.2 us -> 24.6 us (0.976)
  Pallas kernels: 24.3 us -> 23.7 us
    pallas_call x1, Pallas kernels: 21.5 us -> 20.9 us  [body(): pl.pallas_call(functools.partial(loss_kernel, n, widths, turn, after), ou...]
where the time goes in v3:
time: 24.6 us; the launch traced here: 24.4 us
  Pallas kernels  23.7 us (96%)
  between operations  0.64 us (3%)
    pallas_call x1, Pallas kernels, body(): pl.pallas_call(functools.partial(loss_kernel, n, widths, turn, after), ou...  20.9 us
    pallas_call x1, Pallas kernels, body(): pl.pallas_call(store_kernel, out_shape=(*shared, jax.ShapeDtypeStruct((1,...  2.77 us

profile of v3, /device:TPU:0, one launch (start us, length us, event | category | flops | bytes accessed | tf_op | source)
XLA Modules:
  0.0 24.4 jit_solution(2995408836318435503)
XLA Ops:
  0.6 20.9 %shard_map.58 = (bf16[3072,1024]{1,0:T(8,128)(2,1)S(1)}, bf16[8,3072]{1,0:T(8,128)(2,1)S(1)}, f32[8,128]{1,0:T(8,128)S(1)}) custom-call(bf16[8,3072]{1,0:T(8,128)(2,1)} %h_hbm.1, bf16[3072,1024]{1,0:T(8,128)(2,1)} %w_hbm.1, s32[1,64]{1,0:T(1,128)} %bitcast.2), custom_call_target="tpu_custom_call" | custom-call | tf_op jit(solution)/shard_map/pallas_call | solution.py:267
  21.6 2.8 %shard_map.59 = (bf16[3072,1024]{1,0:T(8,128)(2,1)}, bf16[8,3072]{1,0:T(8,128)(2,1)}, f32[1,1]{1,0:T(1,128)}) custom-call(bf16[3072,1024]{1,0:T(8,128)(2,1)S(1)} %get-tuple-element.9.dw_v, bf16[8,3072]{1,0:T(8,128)(2,1)S(1)} %get-tuple-element.10.dh_v, f32[8,128]{1,0:T(8,128)S(1)} %get-tuple-element.11.loss_v), custom_call_target="tpu_custom_call" | custom-call | tf_op jit(solution)/shard_map/pallas_call | solution.py:304

commit v4 on v3

--- a/solution.py
+++ b/solution.py
@@ -10,7 +10,6 @@
 MESH = pl.DeviceIdType.MESH
 F32 = jnp.float32
 BF16 = jnp.bfloat16
-ACROSS = (((1,), (1,)), ((), ()))
 DOWN = (((0,), (0,)), ((), ()))
 
 
@@ -23,7 +22,7 @@
 
 def plan(units):
     if units == 12:
-        return [6, 6], 1, [[], [0, 1]]
+        return [4, 4, 4], 2, [[], [], [0, 1, 2]]
     return [1] * units, 1, [[] if j == 0 else [j - 1] for j in range(units - 1)] + [[units - 2, units - 1] if units > 1 else [0]]
 
 
@@ -35,7 +34,7 @@
 
 def loss_kernel(
     n, widths, turn, after, h_hbm, w_hbm, t_hbm, dw_ref, dh_ref, loss_ref,
-    t_ref, aim_ref, hid_ref, g_ref, w_v, slots, e_v, stats, near, scale, mix, part, xbuf, outb, rbuf,
+    t_ref, aim_ref, hid_ref, g_ref, w_v, turned_v, slots, e_v, stats, near, scale, mix, part, xbuf, outb, rbuf,
     goal, goal_in, goal_sum, goal_far,
     in_sem, w_sem, send_sem, ag_recv, fw_recv, recv_sem, x_recv,
 ):
@@ -92,7 +91,8 @@
     for load in loads:
         load.wait()
     for b in range(blocks):
-        term = lax.dot_general(g_ref[...], w_v[b * tall:(b + 1) * tall, :], ACROSS, preferred_element_type=F32)
+        turned_v[:, b * tall:(b + 1) * tall] = jnp.transpose(w_v[b * tall:(b + 1) * tall, :])
+        term = jnp.dot(g_ref[...], turned_v[:, b * tall:(b + 1) * tall], preferred_element_type=F32)
         for z in range(chips):
             for half in range(2):
                 at = (2 * z + half) * rows
@@ -174,9 +174,7 @@
                     for half in range(2):
                         at = (2 * z + half) * rows
                         scale[i, half, z] = spread[at:at + rows, :]
-        term = lax.dot_general(
-            g_ref[...], w_v[starts[j]:starts[j] + widths[j], :], ACROSS, preferred_element_type=F32
-        )
+        term = jnp.dot(g_ref[...], turned_v[:, starts[j]:starts[j] + widths[j]], preferred_element_type=F32)
         for z in range(chips):
             for half in range(2):
                 at = (2 * z + half) * rows
@@ -275,6 +273,7 @@
             pltpu.VMEM((tokens, depth), BF16),
             pltpu.VMEM((tokens, width), BF16),
             pltpu.VMEM((depth, width), BF16),
+            pltpu.VMEM((width, depth), BF16),
             pltpu.VMEM((pieces, 2, chips, rows, span), BF16),
             pltpu.VMEM((tokens, width), F32),
             pltpu.VMEM((n, 8, tokens), F32),

time: 24.6 us -> 24.6 us (level)
  no operation moved by 1% of the time
where the time goes in v4:
time: 24.6 us; the launch traced here: 24.4 us
  Pallas kernels  23.7 us (96%)
  between operations  0.64 us (3%)
    pallas_call x1, Pallas kernels, body(): pl.pallas_call(functools.partial(loss_kernel, n, widths, turn, after), ou...  20.9 us
    pallas_call x1, Pallas kernels, body(): pl.pallas_call(store_kernel, out_shape=(*shared, jax.ShapeDtypeStruct((1,...  2.77 us

profile of v4, /device:TPU:0, one launch (start us, length us, event | category | flops | bytes accessed | tf_op | source)
XLA Modules:
  0.0 24.4 jit_solution(15412355284345565137)
XLA Ops:
  0.6 20.9 %shard_map.58 = (bf16[3072,1024]{1,0:T(8,128)(2,1)S(1)}, bf16[8,3072]{1,0:T(8,128)(2,1)S(1)}, f32[8,128]{1,0:T(8,128)S(1)}) custom-call(bf16[8,3072]{1,0:T(8,128)(2,1)} %h_hbm.1, bf16[3072,1024]{1,0:T(8,128)(2,1)} %w_hbm.1, s32[1,64]{1,0:T(1,128)} %bitcast.2), custom_call_target="tpu_custom_call" | custom-call | tf_op jit(solution)/shard_map/pallas_call | solution.py:265
  21.6 2.8 %shard_map.59 = (bf16[3072,1024]{1,0:T(8,128)(2,1)}, bf16[8,3072]{1,0:T(8,128)(2,1)}, f32[1,1]{1,0:T(1,128)}) custom-call(bf16[3072,1024]{1,0:T(8,128)(2,1)S(1)} %get-tuple-element.9.dw_v, bf16[8,3072]{1,0:T(8,128)(2,1)S(1)} %get-tuple-element.10.dh_v, f32[8,128]{1,0:T(8,128)S(1)} %get-tuple-element.11.loss_v), custom_call_target="tpu_custom_call" | custom-call | tf_op jit(solution)/shard_map/pallas_call | solution.py:303

commit v5 on v4

--- a/solution.py
+++ b/solution.py
@@ -22,7 +22,7 @@
 
 def plan(units):
     if units == 12:
-        return [4, 4, 4], 2, [[], [], [0, 1, 2]]
+        return [7, 5], 1, [[], [0, 1]]
     return [1] * units, 1, [[] if j == 0 else [j - 1] for j in range(units - 1)] + [[units - 2, units - 1] if units > 1 else [0]]
 
 
@@ -33,7 +33,7 @@
 
 
 def loss_kernel(
-    n, widths, turn, after, h_hbm, w_hbm, t_hbm, dw_ref, dh_ref, loss_ref,
+    n, spans, widths, turn, after, h_hbm, w_hbm, t_hbm, dw_ref, dh_ref, loss_ref,
     t_ref, aim_ref, hid_ref, g_ref, w_v, turned_v, slots, e_v, stats, near, scale, mix, part, xbuf, outb, rbuf,
     goal, goal_in, goal_sum, goal_far,
     in_sem, w_sem, send_sem, ag_recv, fw_recv, recv_sem, x_recv,
@@ -43,7 +43,8 @@
     chip, core = me // 2, me % 2
     away = 1 - core
     partner = chip * 2 + away
-    pieces, rows, span = slots.shape[0], slots.shape[3], slots.shape[4]
+    rows, pieces = slots.shape[2], len(spans)
+    cuts = [sum(spans[:a]) for a in range(pieces)]
     tokens, width = e_v.shape
     depth = w_v.shape[0]
     blocks = split(depth, 6, 256)
@@ -54,19 +55,22 @@
 
     above = chips - 1 - chip
 
+    def cols(a):
+        return pl.ds(cuts[a], spans[a])
+
     def other(k):
         up = (above - k + chips) // chips
         return up * (chips - k) + (1 - up) * (k - 1 - above)
 
     takes = [
-        pltpu.make_async_copy(h_hbm.at[:, pl.ds(a * span, span)], slots.at[a, core, chip], in_sem.at[a])
+        pltpu.make_async_copy(h_hbm.at[:, cols(a)], slots.at[core, chip, :, cols(a)], in_sem.at[a])
         for a in range(pieces)
     ]
     takes.append(pltpu.make_async_copy(t_hbm, t_ref, in_sem.at[pieces]))
     for take in takes:
         take.start()
     loads = [
-        pltpu.make_async_copy(w_hbm.at[pl.ds(a * span, span), :], w_v.at[pl.ds(a * span, span), :], w_sem.at[a])
+        pltpu.make_async_copy(w_hbm.at[cols(a), :], w_v.at[cols(a), :], w_sem.at[a])
         for a in range(pieces)
     ]
 
@@ -81,7 +85,7 @@
     pl.semaphore_wait(barrier, n - 1)
 
     for a in range(pieces):
-        own = slots.at[a, core, chip]
+        own = slots.at[core, chip, :, cols(a)]
         for k in range(1, chips):
             remote(own, own, ag_send, ag_recv.at[a], other(k) * 2 + away).start()
         remote(own, own, ag_send, fw_recv.at[a], partner).start()
@@ -107,23 +111,23 @@
     remote(goal_sum.at[chip], goal_far.at[chip], far_send, far_recv, partner).start()
 
     def finish(a):
-        remote(slots.at[a, core], slots.at[a, core], fw_send, fw_recv.at[a], partner).wait_recv()
-        for z in range(chips):
-            both = jnp.concatenate([slots[a, 0, z].astype(F32), slots[a, 1, z].astype(F32)], axis=0)
-            hid_ref[2 * rows * z:2 * rows * (z + 1), a * span:(a + 1) * span] = both.astype(BF16)
-        term = jnp.dot(
-            hid_ref[:, a * span:(a + 1) * span], w_v[a * span:(a + 1) * span, :], preferred_element_type=F32
-        )
+        at = slice(cuts[a], cuts[a] + spans[a])
+        there = slots.at[core, :, :, cols(a)]
+        remote(there, there, fw_send, fw_recv.at[a], partner).wait_recv()
+        for z in range(chips):
+            both = jnp.concatenate([slots[0, z, :, at].astype(F32), slots[1, z, :, at].astype(F32)], axis=0)
+            hid_ref[2 * rows * z:2 * rows * (z + 1), at] = both.astype(BF16)
+        term = jnp.dot(hid_ref[:, at], w_v[at, :], preferred_element_type=F32)
         if a == 0:
             e_v[...] = term
         else:
             e_v[...] += term
 
     for a in range(pieces):
-        there = slots.at[a, away, pl.ds(0, chips - 1)]
+        there = slots.at[away, pl.ds(0, chips - 1), :, cols(a)]
         remote(there, there, ag_send, ag_recv.at[a], partner).wait_recv()
         for k in range(1, chips):
-            there = slots.at[a, away, other(k)]
+            there = slots.at[away, other(k), :, cols(a)]
             remote(there, there, fw_send, fw_recv.at[a], partner).start()
         if a > 0:
             finish(a - 1)
@@ -225,7 +229,7 @@
         dh_ref[:, at] = (summed + goals * mine[:, chips:chips + 1]).astype(BF16)
 
     for ref, sem in (
-        (slots.at[:, 0], ag_send), (slots.at[:, 0, pl.ds(0, chips - 1)], fw_send), (stats.at[pl.ds(0, n - 1)], st_send),
+        (slots.at[0], ag_send), (slots.at[0, pl.ds(0, chips - 1)], fw_send), (stats.at[pl.ds(0, n - 1)], st_send),
         (near.at[0], near_send), (xbuf, x_send), (rbuf, rs_send), (goal_in, goal_send), (goal_far, far_send),
     ):
         remote(ref, ref, sem, st_recv, partner).wait_send()
@@ -252,18 +256,18 @@
     width = weight.shape[1]
     tokens = rows * n
     chips = n // 2
-    pieces = split(depth, 3, 256)
     unit = depth // split(depth, 12, 128)
     widths, turn, after = plan(depth // unit)
     widths = [w * unit for w in widths]
-    span = depth // pieces
+    spans = [5 * unit, 5 * unit, 2 * unit] if depth == 12 * unit else [depth]
+    pieces = len(spans)
     vmem = pl.BlockSpec(memory_space=pltpu.VMEM)
     dma = pltpu.SemaphoreType.DMA
     hbm = pl.BlockSpec(memory_space=pltpu.HBM)
     shared = (jax.ShapeDtypeStruct((depth, width), BF16), jax.ShapeDtypeStruct((rows, depth), BF16))
     tile = jax.ShapeDtypeStruct((8, 128), F32)
     held = pl.pallas_call(
-        functools.partial(loss_kernel, n, widths, turn, after),
+        functools.partial(loss_kernel, n, spans, widths, turn, after),
         out_shape=(*shared, tile),
         in_specs=[hbm, hbm, hbm],
         out_specs=(vmem, vmem, vmem),
@@ -274,7 +278,7 @@
             pltpu.VMEM((tokens, width), BF16),
             pltpu.VMEM((depth, width), BF16),
             pltpu.VMEM((width, depth), BF16),
-            pltpu.VMEM((pieces, 2, chips, rows, span), BF16),
+            pltpu.VMEM((2, chips, rows, depth), BF16),
             pltpu.VMEM((tokens, width), F32),
             pltpu.VMEM((n, 8, tokens), F32),
             pltpu.VMEM((2, tokens, 128), F32),

time: 24.6 us -> 24.1 us (0.980)
  the two profiles are of different devices: /device:TPU:0 before, /device:TPU:1 now
where the time goes in v5:
time: 24.1 us; the launch traced here: 24 us
  Pallas kernels  23.3 us (97%)
  between operations  0.64 us (3%)
    pallas_call x1, Pallas kernels, body(): pl.pallas_call(functools.partial(loss_kernel, n, spans, widths, turn, aft...  20.6 us
    pallas_call x1, Pallas kernels, body(): pl.pallas_call(store_kernel, out_shape=(*shared, jax.ShapeDtypeStruct((1,...  2.77 us

profile of v5, /device:TPU:1, one launch (start us, length us, event | category | flops | bytes accessed | tf_op | source)
XLA Modules:
  0.0 24.0 jit_solution(1071934642713260551)
XLA Ops:
  0.6 20.6 %shard_map.58 = (bf16[3072,1024]{1,0:T(8,128)(2,1)S(1)}, bf16[8,3072]{1,0:T(8,128)(2,1)S(1)}, f32[8,128]{1,0:T(8,128)S(1)}) custom-call(bf16[8,3072]{1,0:T(8,128)(2,1)} %h_hbm.1, bf16[3072,1024]{1,0:T(8,128)(2,1)} %w_hbm.1, s32[1,64]{1,0:T(1,128)} %bitcast.2), custom_call_target="tpu_custom_call" | custom-call | tf_op jit(solution)/shard_map/pallas_call | solution.py:269
  21.2 2.8 %shard_map.59 = (bf16[3072,1024]{1,0:T(8,128)(2,1)}, bf16[8,3072]{1,0:T(8,128)(2,1)}, f32[1,1]{1,0:T(1,128)}) custom-call(bf16[3072,1024]{1,0:T(8,128)(2,1)S(1)} %get-tuple-element.9.dw_v, bf16[8,3072]{1,0:T(8,128)(2,1)S(1)} %get-tuple-element.10.dh_v, f32[8,128]{1,0:T(8,128)S(1)} %get-tuple-element.11.loss_v), custom_call_target="tpu_custom_call" | custom-call | tf_op jit(solution)/shard_map/pallas_call | solution.py:307
